TPU v7x, 128 devices: a whole 4x4x4 slice. The times are simulated.
128 devices in a mesh: row: 8 (over x_hi, z), col: 16 (over x_lo, y, core).
Axes of the slice: x: 4 (x_hi: 2, x_lo: 2; x = x_hi * 2 + x_lo), y: 4, z: 4, core: 2. Of those that a mesh axis runs over, the one named last changes fastest.
Arguments:
- tokens: bfloat16 [1024, 12288], P('row', 'col'), may hold values from -6 to 6
- prev_tokens: bfloat16 [1024, 12288], P('row', 'col'), may hold values from -6 to 6
- hidden_grad: bfloat16 [1024, 49152], P('col', 'row'), may hold values from -6 to 6
- active_blocks: int32 [1], replicated, may hold values from 6 to 16
- weight: bfloat16 [12288, 49152], P('col', 'row'), may hold values from -0.0546875 to 0.0546875
Outputs:
- activation: bfloat16 [1024, 49152], P('col', 'row')
- weight_grad: bfloat16 [12288, 49152], P('col', 'row')
Inputs may be any that keep to these rules, and one draw needn't show every extreme that they name: The sampled blocks are the first active_blocks[0] blocks of 3072 hidden units.
All inputs are finite; a program needn't handle non-finite values.
Results may differ from a plain program's by a relative error of at most 0.001.
Values may be sent and summed in bfloat16 or wider, within the bound.
A program may use at most 640 MiB of HBM per device.

v0:
```python
import jax
import jax.numpy as jnp
from jax import lax
from jax.sharding import PartitionSpec as P

BLOCK = 3072


def in_one_piece(arrays, axis, dim, along):
    both = jnp.concatenate(arrays, axis=along)
    result, at, outs = (lax.all_gather(both, axis, axis=dim, tiled=True), 0, [])
    for a in arrays:
        outs.append(lax.slice_in_dim(result, at, at + a.shape[along], axis=along))
        at += a.shape[along]
    return tuple(outs)


def shards(tokens, prev_tokens, hidden_grad, active_blocks, weight):
    local_units = weight.shape[1]
    first_unit = lax.axis_index("row") * local_units
    unit_limit = active_blocks[0] * BLOCK
    unit_ids = first_unit + lax.iota(jnp.int32, local_units)
    unit_mask = (unit_ids < unit_limit).astype(jnp.float32)
    gathered, earlier = in_one_piece((tokens, prev_tokens), "row", 0, 1)
    hidden = lax.psum_scatter(
        jnp.dot(gathered, weight, preferred_element_type=jnp.float32),
        "col",
        scatter_dimension=0,
        tiled=True,
    )
    activation = (jax.nn.gelu(hidden, approximate=False) * unit_mask).astype(jnp.bfloat16)
    grad_sum = lax.dot_general(
        earlier,
        lax.all_gather(hidden_grad, "col", axis=0, tiled=True),
        (((0,), (0,)), ((), ())),
        preferred_element_type=jnp.float32,
    )
    weight_grad = (grad_sum * unit_mask).astype(jnp.bfloat16)
    return (activation, weight_grad)


def solution(mesh):
    return jax.shard_map(
        shards,
        mesh=mesh,
        in_specs=(P("row", "col"), P("row", "col"), P("col", "row"), P(), P("col", "row")),
        out_specs=(P("col", "row"), P("col", "row")),
        check_vma=False,
    )
```

profile of v0, /device:TPU:0, one launch (start us, length us, event | category | flops | bytes accessed | tf_op | source)
XLA Modules:
  0.0 303.0 jit_solution(265817429871638443)
XLA Ops:
  7.2 0.0 all-gather.3.cloned.1.call-start
  7.2 1.8 pad_maximum_fusion
  9.0 0.0 all-gather.3.cloned.1.call-update
  9.0 0.0 all-gather.5.cloned.1.call-start
  9.1 0.7 all-gather.5.cloned.1.call-update
  9.8 0.0 reduce-scatter.2.cloned.1.call-start
  9.8 66.0 %all-gather.3.cloned.1.call-done = bf16[1024,1536]{1,0:T(8,128)(2,1)} async-done(((bf16[128,1536]{1,0:T(8,128)(2,1)}), bf16[1024,1536]{1,0:T(8,128)(2,1)}) %all-gather.3.cloned.1.call-update) | async-done | bytes 3145744 | tf_op jit(solution)/shard_map/all_gather | solution.py:11
  75.8 17.5 %fusion.5 = f32[1024,6144]{1,0:T(8,128)} fusion(bf16[768,6144]{1,0:T(8,128)(2,1)} %param.9, bf16[1024,1536]{1,0:T(8,128)(2,1)} %all-gather.3.cloned.1.call-done), kind=kOutput, calls=%fused_computation.7 | convolution fusion | flops 9663676416 | bytes 36175872 | tf_op jit(solution)/shard_map/dot_general | solution.py:26
  93.3 0.0 copy-start
  93.3 0.0 reduce-scatter.2.cloned.1.call-update
  94.2 52.9 %all-gather.5.cloned.1.call-done = bf16[1024,6144]{1,0:T(8,128)(2,1)} async-done(((bf16[64,6144]{1,0:T(8,128)(2,1)}), bf16[1024,6144]{1,0:T(8,128)(2,1)}) %all-gather.5.cloned.1.call-update) | async-done | bytes 12582928 | tf_op jit(solution)/shard_map/all_gather | solution.py:34
  147.1 0.0 copy-done
  147.1 16.8 %multiply_convert_fusion = bf16[768,6144]{1,0:T(8,128)(2,1)} fusion(bf16[1024,6144]{1,0:T(8,128)(2,1)} %all-gather.5.cloned.1.call-done, f32[6144]{0:T(1024)S(1)} %fusion.14, bf16[1024,1536]{1,0:T(8,128)(2,1)S(1)} %copy-done), kind=kOutput, calls=%fused_computation | convolution fusion | flops 9673113600 | bytes 23617536 | tf_op jit(solution)/shard_map/dot_general | solution.py:32
  163.8 127.4 %reduce-scatter.2.cloned.1.call-done = f32[64,6144]{1,0:T(8,128)} async-done(((f32[1024,6144]{1,0:T(8,128)}), f32[64,6144]{1,0:T(8,128)}) %reduce-scatter.2.cloned.1.call-update) | async-done | bytes 1572880 | tf_op jit(solution)/shard_map/reduce_scatter | solution.py:25
  291.2 5.3 %fusion.3 = bf16[64,6144]{1,0:T(8,128)(2,1)} fusion(f32[64,6144]{1,0:T(8,128)} %reduce-scatter.2.cloned.1.call-done, f32[6144]{0:T(1024)S(1)} %fusion.14), kind=kLoop, calls=%fused_computation.5 | loop fusion | flops 25952256 | bytes 2383872 | tf_op jit(solution)/shard_map/convert_element_type | solution.py:31
  (1 shorter events, 0.0 us)
Async XLA Ops:
  7.2 68.6 %all-gather.3.cloned.1.call-start = ((), (), s32[]{:S(2)}) async-start(), calls=%async_computation.1 | async-start | bytes 3538944 | tf_op jit(solution)/shard_map/all_gather | solution.py:11
  9.0 138.0 %all-gather.5.cloned.1.call-start = ((), (), s32[]{:S(2)}) async-start(), calls=%async_computation.3 | async-start | bytes 13369344 | tf_op jit(solution)/shard_map/all_gather | solution.py:34
  9.8 281.4 %reduce-scatter.2.cloned.1.call-start = ((), (), s32[]{:S(2)}) async-start(), calls=%async_computation.2 | async-start | bytes 26738688 | tf_op jit(solution)/shard_map/reduce_scatter | solution.py:25
  93.3 53.7 %copy-start = (bf16[1024,1536]{1,0:T(8,128)(2,1)S(1)}, bf16[1024,1536]{1,0:T(8,128)(2,1)}, u32[]{:S(2)}) copy-start(bf16[1024,1536]{1,0:T(8,128)(2,1)} %all-gather.3.cloned.1.call-done) | copy-start | bytes 9437188
Sparse Core Ops, SparseCore 0:
  10.8 64.8 all-gather.2
  77.5 69.5 all-gather.4
  149.5 141.6 reduce-scatter.1
where the time goes:
time: 303 us
  waiting for transfers between devices  247 us (82%)
  matrix products  34.3 us (11%)
  between operations  14.6 us (5%)
  other arithmetic  7.08 us (2%)
    reduce_scatter x1, waiting for transfers between devices, shards(): lax.psum_scatter(jnp.dot(gathered, weight, preferred_element_type=jnp.flo...  127 us
    all_gather x1, waiting for transfers between devices, in_one_piece(): result, at, outs = (lax.all_gather(both, axis, axis=dim, tiled=True), 0, [])  66 us
    all_gather x1, waiting for transfers between devices, shards(): lax.all_gather(hidden_grad, 'col', axis=0, tiled=True)  52.9 us
    dot_general x1, matrix products, shards(): jnp.dot(gathered, weight, preferred_element_type=jnp.float32)  17.5 us
    dot_general x1, matrix products, shards(): lax.dot_general(earlier, lax.all_gather(hidden_grad, 'col', axis=0, tiled...  16.8 us
  transfers between devices with their start and end apart: 3, of which 3 were waited for; matrix products, arithmetic and copies ran while one was open for 11% of the time, Pallas kernels for 0%

commit v1 on v0

--- a/solution.py
+++ b/solution.py
@@ -31,7 +31,9 @@
     activation = (jax.nn.gelu(hidden, approximate=False) * unit_mask).astype(jnp.bfloat16)
     grad_sum = lax.dot_general(
         earlier,
-        lax.all_gather(hidden_grad, "col", axis=0, tiled=True),
+        jnp.concatenate(
+            lax.all_to_all(jnp.stack([hidden_grad] * lax.axis_size("col")), "col", 0, 0), axis=0
+        ),
         (((0,), (0,)), ((), ())),
         preferred_element_type=jnp.float32,
     )

time: 303 us -> 401 us (1.32)
  waiting for transfers between devices: 247 us -> 331 us
  local copies, waits for them, and re-layouts: 0.01 us -> 7.98 us
  starting transfers between devices: 0.12 us -> 5.33 us
    all_to_all x0 -> x1, waiting for transfers between devices: none -> 220 us  [shards(): lax.all_to_all(jnp.stack([hidden_grad] * lax.axis_size('col')), 'col', 0, 0)]
    reduce_scatter x1, waiting for transfers between devices: 127 us -> 44.6 us  [shards(): lax.psum_scatter(jnp.dot(gathered, weight, preferred_element_type=jnp.flo...]
    all_gather x1 -> x0, waiting for transfers between devices: 52.9 us -> none  [shards(): lax.all_gather(hidden_grad, 'col', axis=0, tiled=True)]
    another operation x0 -> x1, local copies, waits for them, and re-layouts: none -> 6.86 us  [shards(): jnp.stack([hidden_grad] * lax.axis_size('col'))]
    all_to_all x0 -> x1, starting transfers between devices: none -> 5.25 us  [shards(): lax.all_to_all(jnp.stack([hidden_grad] * lax.axis_size('col')), 'col', 0, 0)]
  transfers between devices with their start and end apart: 3 -> 3, of which waited for: 3 -> 3; matrix products, arithmetic and copies ran while one was open for 11% -> 6% of each run, Pallas kernels for 0% -> 0%
where the time goes in v1:
time: 401 us
  waiting for transfers between devices  331 us (83%)
  matrix products  34.5 us (9%)
  between operations  14.7 us (4%)
  local copies, waits for them, and re-layouts  7.98 us (2%)
  other arithmetic  7.08 us (2%)
  starting transfers between devices  5.33 us (1%)
    all_to_all x1, waiting for transfers between devices, shards(): lax.all_to_all(jnp.stack([hidden_grad] * lax.axis_size('col')), 'col', 0, 0)  220 us
    all_gather x1, waiting for transfers between devices, in_one_piece(): result, at, outs = (lax.all_gather(both, axis, axis=dim, tiled=True), 0, [])  66.7 us
    reduce_scatter x1, waiting for transfers between devices, shards(): lax.psum_scatter(jnp.dot(gathered, weight, preferred_element_type=jnp.flo...  44.6 us
    dot_general x1, matrix products, shards(): jnp.dot(gathered, weight, preferred_element_type=jnp.float32)  17.5 us
    dot_general x1, matrix products, shards(): lax.dot_general(earlier, jnp.concatenate(lax.all_to_all(jnp.stack([hidden...  16.9 us
  transfers between devices with their start and end apart: 3, of which 3 were waited for; matrix products, arithmetic and copies ran while one was open for 6% of the time, Pallas kernels for 0%

profile of v1, /device:TPU:0, one launch (start us, length us, event | category | flops | bytes accessed | tf_op | source)
XLA Modules:
  0.0 401.0 jit_solution(17682584979167287456)
XLA Ops:
  7.2 0.0 all-gather.2.cloned.1.call-start
  7.2 1.8 pad_maximum_fusion
  9.0 0.0 all-gather.2.cloned.1.call-update
  9.0 0.0 reduce-scatter.2.cloned.1.call-start
  9.1 66.7 %all-gather.2.cloned.1.call-done = bf16[1024,1536]{1,0:T(8,128)(2,1)} async-done(((bf16[128,1536]{1,0:T(8,128)(2,1)}), bf16[1024,1536]{1,0:T(8,128)(2,1)}) %all-gather.2.cloned.1.call-update) | async-done | bytes 3145744 | tf_op jit(solution)/shard_map/all_gather | solution.py:11
  75.8 17.5 %fusion.5 = f32[1024,6144]{1,0:T(8,128)} fusion(bf16[768,6144]{1,0:T(8,128)(2,1)} %param.9, bf16[1024,1536]{1,0:T(8,128)(2,1)} %all-gather.2.cloned.1.call-done), kind=kOutput, calls=%fused_computation.7 | convolution fusion | flops 9663676416 | bytes 36175872 | tf_op jit(solution)/shard_map/dot_general | solution.py:26
  93.3 0.0 copy-start
  93.3 0.0 reduce-scatter.2.cloned.1.call-update
  93.4 1.1 copy-done
  94.5 6.9 %stack.2 = bf16[16,64,6144]{2,1,0:T(8,128)(2,1)} broadcast(bf16[64,6144]{1,0:T(8,128)(2,1)S(1)} %copy-done), dimensions={1,2} | broadcast | bytes 13369344 | tf_op jit(solution)/shard_map/stack | solution.py:35
  101.3 0.0 copy-start.1
  101.3 5.3 %all-to-all-start = ((bf16[16,64,6144]{2,1,0:T(8,128)(2,1)}), bf16[16,64,6144]{2,1,0:T(8,128)(2,1)}, u32[]{:S(2)}, u32[]{:S(2)}) async-start(bf16[16,64,6144]{2,1,0:T(8,128)(2,1)} %stack.2), calls=%async_computation.1 | async-start | bytes 25165824 | tf_op jit(solution)/shard_map/all_to_all | solution.py:35
  107.3 220.2 %all-to-all-done = bf16[16,64,6144]{2,1,0:T(8,128)(2,1)} async-done(((bf16[16,64,6144]{2,1,0:T(8,128)(2,1)}), bf16[16,64,6144]{2,1,0:T(8,128)(2,1)}, u32[]{:S(2)}, u32[]{:S(2)}) %all-to-all-start) | async-done | bytes 12582944 | tf_op jit(solution)/shard_map/all_to_all | solution.py:35
  327.4 0.0 copy-done.1
  327.4 16.9 %multiply_convert_fusion = bf16[768,6144]{1,0:T(8,128)(2,1)} fusion(bf16[1024,6144]{1,0:T(8,128)(2,1)} %bitcast.1, f32[6144]{0:T(1024)S(1)} %fusion.14, bf16[1024,1536]{1,0:T(8,128)(2,1)S(1)} %copy-done.1), kind=kOutput, calls=%fused_computation | convolution fusion | flops 9673113600 | bytes 23617536 | tf_op jit(solution)/shard_map/dot_general | solution.py:32
  344.3 44.6 %reduce-scatter.2.cloned.1.call-done = f32[64,6144]{1,0:T(8,128)} async-done(((f32[1024,6144]{1,0:T(8,128)}), f32[64,6144]{1,0:T(8,128)}) %reduce-scatter.2.cloned.1.call-update) | async-done | bytes 1572880 | tf_op jit(solution)/shard_map/reduce_scatter | solution.py:25
  388.9 5.3 %fusion.3 = bf16[64,6144]{1,0:T(8,128)(2,1)} fusion(f32[64,6144]{1,0:T(8,128)} %reduce-scatter.2.cloned.1.call-done, f32[6144]{0:T(1024)S(1)} %fusion.14), kind=kLoop, calls=%fused_computation.5 | loop fusion | flops 25952256 | bytes 2383872 | tf_op jit(solution)/shard_map/convert_element_type | solution.py:31
  (1 shorter events, 0.0 us)
Async XLA Ops:
  7.2 68.6 %all-gather.2.cloned.1.call-start = ((), (), s32[]{:S(2)}) async-start(), calls=%async_computation.2 | async-start | bytes 3538944 | tf_op jit(solution)/shard_map/all_gather | solution.py:11
  9.0 379.9 %reduce-scatter.2.cloned.1.call-start = ((), (), s32[]{:S(2)}) async-start(), calls=%async_computation.3 | async-start | bytes 26738688 | tf_op jit(solution)/shard_map/reduce_scatter | solution.py:25
  93.3 1.1 copy-start
  101.3 226.1 %copy-start.1 = (bf16[1024,1536]{1,0:T(8,128)(2,1)S(1)}, bf16[1024,1536]{1,0:T(8,128)(2,1)}, u32[]{:S(2)}) copy-start(bf16[1024,1536]{1,0:T(8,128)(2,1)} %all-gather.2.cloned.1.call-done) | copy-start | bytes 9437188
  101.3 226.1 %all-to-all-start = ((bf16[16,64,6144]{2,1,0:T(8,128)(2,1)}), bf16[16,64,6144]{2,1,0:T(8,128)(2,1)}, u32[]{:S(2)}, u32[]{:S(2)}) async-start(bf16[16,64,6144]{2,1,0:T(8,128)(2,1)} %stack.2), calls=%async_computation.1 | async-start | bytes 25165824 | tf_op jit(solution)/shard_map/all_to_all | solution.py:35
Sparse Core Ops, SparseCore 0:
  10.8 64.8 all-gather.1
  93.5 295.4 reduce-scatter.1
